TPU v7x, 32 devices: a whole 2x2x4 slice. The times are simulated.
32 devices in a mesh: dp: 8 (over z, y), tensor: 4 (over x, core).
Axes of the slice: x: 2, y: 2, z: 4, core: 2. Of those that a mesh axis runs over, the one named last changes fastest.
Arguments:
- tokens: bfloat16 [32768, 1024], P(('dp', 'tensor')), may hold values from -6 to 6
- segments: int32 [64, 512], P(('dp', 'tensor')), may hold values from 0 to 1, as said below
- lengths: int32 [64], P(('dp', 'tensor')), may hold values from 128 to 512, as said below
- type_table: bfloat16 [2, 1024], replicated, may hold values from -3 to 3
- attn_weight: bfloat16 [3145728], P(('dp', 'tensor')), may hold values from -0.1875 to 0.1875
- out_weight: bfloat16 [1048576], P(('dp', 'tensor')), may hold values from -0.75 to 0.75
- ffn_in_weight: bfloat16 [1024, 4096], P('dp', 'tensor'), may hold values from -0.1875 to 0.1875
- ffn_out_weight: bfloat16 [4096, 1024], P('tensor', 'dp'), may hold values from -0.125 to 0.125
- attn_bias: bfloat16 [3, 1024], replicated, may hold values from -3 to 3
- ffn_bias_in: bfloat16 [4096], replicated, may hold values from -3 to 3
- ffn_bias_out: bfloat16 [1024], replicated, may hold values from -3 to 3
- norm_gain: bfloat16 [2, 1024], replicated, may hold values from 0.099609375 to 1.8984375
- norm_shift: bfloat16 [2, 1024], replicated, may hold values from -3 to 3
- cotangent: bfloat16 [32768, 1024], P(('dp', 'tensor')), may hold values from -6 to 6
Outputs:
- output: bfloat16 [32768, 1024], P(('dp', 'tensor'))
- grad_input: bfloat16 [32768, 1024], P(('dp', 'tensor'))
- attn_bias_grad: float32 [3, 1024], replicated
- ffn_bias_in_grad: float32 [4096], replicated
- ffn_bias_out_grad: float32 [1024], replicated
- norm_gain_grad: float32 [2, 1024], replicated
- norm_shift_grad: float32 [2, 1024], replicated
Inputs may be any that keep to these rules, and one draw needn't show every extreme that they name: `lengths`: the valid tokens of a sequence are its first ones; in every draw some sequence has all 512 valid. `segments`: segment id 0 up to and including a separator at position 1 to length - 2, 1 after it up to the sequence's length, 0 on padding.
All inputs are finite; a program needn't handle non-finite values.
Results may differ from a plain program's by a relative error of at most 0.015.
Values may be sent and summed in bfloat16 or wider, within the bound.
A program may use at most 192 MiB of HBM per device.

v0:
```python
from functools import partial
import math
import jax
import jax.numpy as jnp
from jax import lax
from jax.sharding import PartitionSpec as P

HEADS = 16
HEAD = 64


def matmul(left_side, right_side):
    return jnp.dot(left_side, right_side, preferred_element_type=jnp.float32)


def matmul_t(left_side, right_side):
    return lax.dot_general(
        left_side, right_side, (((1,), (1,)), ((), ())), preferred_element_type=jnp.float32
    )


def norm_forward(residual, gain_row, shift_row):
    row_mean = jnp.mean(residual, axis=-1, keepdims=True)
    centered = residual - row_mean
    inverse = lax.rsqrt(jnp.mean(centered * centered, axis=-1, keepdims=True) + 1e-12)
    normed = centered * inverse
    return (normed * gain_row + shift_row, normed, inverse)


def norm_backward(upstream, normed, inverse, gain_row):
    scaled = upstream * gain_row
    inner = (
        scaled
        - jnp.mean(scaled, axis=-1, keepdims=True)
        - normed * jnp.mean(scaled * normed, axis=-1, keepdims=True)
    )
    return (inner * inverse, jnp.sum(upstream * normed, axis=0), jnp.sum(upstream, axis=0))


def gelu_slope(preact):
    normal_cdf = 0.5 * (1.0 + jax.scipy.special.erf(preact * 0.7071067811865476))
    normal_pdf = jnp.exp(-0.5 * preact * preact) * 0.3989422804014327
    return normal_cdf + preact * normal_pdf


def score_block(queries, key_rows, key_valid, score_scale):
    scores = (
        jnp.einsum("qhd,khd->hqk", queries, key_rows, preferred_element_type=jnp.float32)
        * score_scale
    )
    return jnp.where(key_valid[None, None, :], scores, -1000000000.0)


def context_block(block_items, score_scale):
    queries, key_rows, value_rows, key_valid = block_items
    masked = score_block(queries, key_rows, key_valid, score_scale)
    row_max = jnp.max(masked, axis=-1, keepdims=True)
    log_total = row_max + jnp.log(jnp.sum(jnp.exp(masked - row_max), axis=-1, keepdims=True))
    attn_prob = jnp.exp(masked - log_total)
    context = jnp.einsum(
        "hqk,khd->qhd",
        attn_prob.astype(jnp.bfloat16),
        value_rows,
        preferred_element_type=jnp.float32,
    )
    return (context.astype(jnp.bfloat16), log_total)


def gradient_block(block_items, score_scale):
    queries, key_rows, value_rows, key_valid, log_total, d_context = block_items
    masked = score_block(queries, key_rows, key_valid, score_scale)
    attn_prob = jnp.exp(masked - log_total)
    d_prob = jnp.einsum("qhd,khd->hqk", d_context, value_rows, preferred_element_type=jnp.float32)
    d_values = jnp.einsum(
        "hqk,qhd->khd",
        attn_prob.astype(jnp.bfloat16),
        d_context,
        preferred_element_type=jnp.float32,
    )
    row_dot = jnp.sum(d_prob * attn_prob, axis=-1, keepdims=True)
    d_scores = (attn_prob * (d_prob - row_dot)).astype(jnp.bfloat16)
    d_queries = (
        jnp.einsum("hqk,khd->qhd", d_scores, key_rows, preferred_element_type=jnp.float32)
        * score_scale
    )
    d_keys = (
        jnp.einsum("hqk,qhd->khd", d_scores, queries, preferred_element_type=jnp.float32)
        * score_scale
    )
    return (
        d_queries.astype(jnp.bfloat16),
        d_keys.astype(jnp.bfloat16),
        d_values.astype(jnp.bfloat16),
    )


def per_device(
    tokens,
    segments,
    lengths,
    type_table,
    attn_weight,
    out_weight,
    ffn_in_weight,
    ffn_out_weight,
    attn_bias,
    ffn_bias_in,
    ffn_bias_out,
    norm_gain,
    norm_shift,
    cotangent,
):
    tok_rows, model_width = tokens.shape
    seq_count, seq_len = segments.shape
    score_scale = 1.0 / math.sqrt(HEAD)
    bias_attn = attn_bias.astype(jnp.float32)
    bias_first = ffn_bias_in.astype(jnp.float32)
    bias_second = ffn_bias_out.astype(jnp.float32)
    gain_rows = norm_gain.astype(jnp.float32)
    shift_rows = norm_shift.astype(jnp.float32)
    qkv_flat, out_flat = (
        lax.all_gather(attn_weight, ("dp", "tensor"), axis=0, tiled=True),
        lax.all_gather(out_weight, ("dp", "tensor"), axis=0, tiled=True),
    )
    projections = qkv_flat.reshape(3, model_width, model_width)
    out_proj = out_flat.reshape(model_width, model_width)
    w_first, w_second = (
        lax.all_gather(ffn_in_weight, "dp", axis=0, tiled=True),
        lax.all_gather(ffn_out_weight, "dp", axis=1, tiled=True),
    )
    w_first, w_second = (
        lax.all_gather(w_first, "tensor", axis=1, tiled=True),
        lax.all_gather(w_second, "tensor", axis=0, tiled=True),
    )
    table_rows = type_table.astype(jnp.float32)
    type_rows = jnp.where(
        (segments.reshape(-1) == 1)[:, None], table_rows[1][None, :], table_rows[0][None, :]
    )
    block_input = tokens.astype(jnp.float32) + type_rows
    lowered = block_input.astype(jnp.bfloat16)
    projected = jnp.einsum("td,mde->mte", lowered, projections, preferred_element_type=jnp.float32)
    queries = (projected[0] + bias_attn[0]).astype(jnp.bfloat16)
    key_rows = projected[1].astype(jnp.bfloat16)
    value_rows = (projected[2] + bias_attn[1]).astype(jnp.bfloat16)
    head_shape = (seq_count, seq_len, HEADS, HEAD)
    query_heads = queries.reshape(head_shape)
    key_heads = key_rows.reshape(head_shape)
    value_heads = value_rows.reshape(head_shape)
    key_valid = jnp.arange(seq_len, dtype=jnp.int32)[None, :] < lengths[:, None]
    context, log_total = lax.map(
        partial(context_block, score_scale=score_scale),
        (query_heads, key_heads, value_heads, key_valid),
    )
    context = context.reshape(tok_rows, model_width)
    attn_out = matmul(context, out_proj) + bias_attn[2]
    middle, normed_one, inverse_one = norm_forward(
        block_input + attn_out, gain_rows[0], shift_rows[0]
    )
    middle_low = middle.astype(jnp.bfloat16)
    preact = matmul(middle_low, w_first) + bias_first
    hidden = jax.nn.gelu(preact, approximate=False).astype(jnp.bfloat16)
    ffn_out = matmul(hidden, w_second) + bias_second
    output_rows, normed_two, inverse_two = norm_forward(
        middle + ffn_out, gain_rows[1], shift_rows[1]
    )
    output = output_rows.astype(jnp.bfloat16)
    qkv_again, out_again = (
        lax.all_gather(attn_weight, ("dp", "tensor"), axis=0, tiled=True),
        lax.all_gather(out_weight, ("dp", "tensor"), axis=0, tiled=True),
    )
    projections = qkv_again.reshape(3, model_width, model_width)
    out_proj = out_again.reshape(model_width, model_width)
    w_first, w_second = (
        lax.all_gather(ffn_in_weight, "dp", axis=0, tiled=True),
        lax.all_gather(ffn_out_weight, "dp", axis=1, tiled=True),
    )
    w_first, w_second = (
        lax.all_gather(w_first, "tensor", axis=1, tiled=True),
        lax.all_gather(w_second, "tensor", axis=0, tiled=True),
    )
    d_second_sum, gain_two_grad, shift_two_grad = norm_backward(
        cotangent.astype(jnp.float32), normed_two, inverse_two, gain_rows[1]
    )
    d_ffn = d_second_sum.astype(jnp.bfloat16)
    bias_out_grad = jnp.sum(d_ffn.astype(jnp.float32), axis=0)
    d_preact = (matmul_t(d_ffn, w_second) * gelu_slope(preact)).astype(jnp.bfloat16)
    bias_in_grad = jnp.sum(d_preact.astype(jnp.float32), axis=0)
    d_middle_ffn = matmul_t(d_preact, w_first)
    d_middle = d_second_sum + d_middle_ffn
    d_first_sum, gain_one_grad, shift_one_grad = norm_backward(
        d_middle, normed_one, inverse_one, gain_rows[0]
    )
    d_attn = d_first_sum.astype(jnp.bfloat16)
    bias_o_grad = jnp.sum(d_attn.astype(jnp.float32), axis=0)
    d_context = matmul_t(d_attn, out_proj).astype(jnp.bfloat16).reshape(head_shape)
    d_queries, d_keys, d_values = lax.map(
        partial(gradient_block, score_scale=score_scale),
        (query_heads, key_heads, value_heads, key_valid, log_total, d_context),
    )
    d_queries = d_queries.reshape(tok_rows, model_width)
    d_keys = d_keys.reshape(tok_rows, model_width)
    d_values = d_values.reshape(tok_rows, model_width)
    bias_q_grad = jnp.sum(d_queries.astype(jnp.float32), axis=0)
    bias_v_grad = jnp.sum(d_values.astype(jnp.float32), axis=0)
    stacked = jnp.stack([d_queries, d_keys, d_values])
    d_input = d_first_sum + jnp.einsum(
        "mte,mde->td", stacked, projections, preferred_element_type=jnp.float32
    )
    grad_input = d_input.astype(jnp.bfloat16)
    attn_grad = jnp.stack([bias_q_grad, bias_v_grad, bias_o_grad])
    gain_grad = jnp.stack([gain_one_grad, gain_two_grad])
    shift_grad = jnp.stack([shift_one_grad, shift_two_grad])
    attn_grad, bias_in_grad, bias_out_grad, gain_grad, shift_grad = lax.psum(
        (attn_grad, bias_in_grad, bias_out_grad, gain_grad, shift_grad), ("dp", "tensor")
    )
    return (output, grad_input, attn_grad, bias_in_grad, bias_out_grad, gain_grad, shift_grad)


def solution(mesh):
    in_specs = (
        P(("dp", "tensor"), None),
        P(("dp", "tensor"), None),
        P(("dp", "tensor")),
        P(),
        P(("dp", "tensor")),
        P(("dp", "tensor")),
        P("dp", "tensor"),
        P("tensor", "dp"),
        P(),
        P(),
        P(),
        P(),
        P(),
        P(("dp", "tensor"), None),
    )
    out_specs = (P(("dp", "tensor"), None), P(("dp", "tensor"), None), P(), P(), P(), P(), P())
    return jax.shard_map(
        per_device, mesh=mesh, in_specs=in_specs, out_specs=out_specs, check_vma=False
    )
```

profile of v0, /device:TPU:0, one launch (start us, length us, event | category | flops | bytes accessed | tf_op | source)
XLA Modules:
  0.0 693.1 jit_solution(5041062795089590468)
XLA Ops:
  10.0 51.9 %all-gather.11.cloned.1.call-done = bf16[1024,1024]{1,0:T(8,128)(2,1)} async-done(((bf16[128,1024]{1,0:T(8,128)(2,1)}), bf16[1024,1024]{1,0:T(8,128)(2,1)}) %all-gather.11.cloned.1.call-update) | async-done | bytes 2097168 | tf_op jit(solution)/shard_map/all_gather | solution.py:128
  63.5 2.6 copy.75
  67.5 3.9 copy.85
  72.7 40.2 %all-gather.15.cloned.1.call-done = bf16[1024,1024]{1,0:T(8,128)(2,1)} async-done(((bf16[1024,128]{1,0:T(8,128)(2,1)}), bf16[1024,1024]{1,0:T(8,128)(2,1)}) %all-gather.15.cloned.1.call-update) | async-done | bytes 2097168 | tf_op jit(solution)/shard_map/all_gather | solution.py:129
  113.0 57.3 %all-gather.9.cloned.1.call-done = bf16[1048576]{0:T(1024)(128)(2,1)} async-done(((bf16[32768]{0:T(1024)(128)(2,1)}), bf16[1048576]{0:T(1024)(128)(2,1)}) %all-gather.9.cloned.1.call-update) | async-done | bytes 2097168 | tf_op jit(solution)/shard_map/all_gather | solution.py:123
  170.2 4.1 reshape.135
  174.4 66.6 %all-gather.7.cloned.1.call-done = bf16[3145728]{0:T(1024)(128)(2,1)} async-done(((bf16[98304]{0:T(1024)(128)(2,1)}), bf16[3145728]{0:T(1024)(128)(2,1)}) %all-gather.7.cloned.1.call-update) | async-done | bytes 6291472 | tf_op jit(solution)/shard_map/all_gather | solution.py:122
  241.0 10.6 %reshape.133 = bf16[3,1024,1024]{2,1,0:T(8,128)(2,1)} reshape(bf16[3145728]{0:T(1024)(128)(2,1)} %all-gather.7.cloned.1.call-done) | data formatting | bytes 12582912 | tf_op jit(solution)/shard_map/reshape | solution.py:125
  251.5 11.7 %convolution_bitcast_fusion = f32[3,1024,1024]{2,1,0:T(8,128)S(1)} fusion(bf16[3,1024,1024]{2,1,0:T(8,128)(2,1)} %reshape.133, bf16[1024,1024]{0,1:T(8,128)(2,1)S(1)} %copy-done.22, f32[1024]{0:T(1024)S(1)} %bitcast.169, f32[1024]{0:T(1024)S(1)} %bitcast.167, pred[1024]{0:T(1024)(128)(4,1)S(1)} %eq.15), kind=kOutput, calls=%fused_computation.99 | convolution fusion | flops 6446645248 | bytes 20980736 | tf_op jit(solution)/shard_map/td,mde->mte/dot_general | solution.py:141
  263.5 4.1 fusion.135
  267.7 5.4 copy.77
  273.1 6.6 squeeze.34
  279.7 3.9 add_convert_fusion.2
  283.6 1.8 copy.80
  285.4 5.4 copy.78
  290.8 6.6 squeeze.35
  297.4 3.9 add_convert_fusion.1
  301.3 1.8 copy.81
  303.2 4.0 reshape.143
  307.2 4.9 copy.82
  313.7 28.0 %while.26 = (s32[]{:T(128)}, bf16[2,512,16,64]{1,3,2,0:T(8,128)(2,1)}, f32[2,16,512,1]{2,1,3,0:T(8,128)S(1)}, bf16[2,512,16,64]{1,3,2,0:T(8,128)(2,1)}, pred[2,5...) while((s32[]{:T(128)}, ...), condition=%wide.region_3.4_spmd, body=%wide.region_0.3_spmd.sunk | while | flops 1120395264 | bytes 63181432 | solution.py:150
  313.7 5.1 fusion.169
  318.8 3.8 exponential_reduce_fusion.2
  322.7 4.8 fusion.170
  327.5 5.0 fusion.169
  332.5 3.8 exponential_reduce_fusion.2
  336.4 4.8 fusion.170
  341.7 4.6 copy.83
  346.9 3.0 fusion.139
  349.9 1.9 copy-done.11
  352.3 16.8 %fusion.90 = f32[1024,4096]{1,0:T(8,128)} fusion(bf16[1024,4096]{1,0:T(8,128)(2,1)} %all-gather.13.cloned.1.call-done, f32[1024,1024]{0,1:T(8,128)} %copy-done.11, f32[1024]{0:T(1024)S(1)} %bitcast.165, f32[1024]{0:T(1024)S(1)} %bitcast.156, f32[1024]{0:T(1024)S(1)} %add_rsqrt_fusion.1, f32[1024]{0:T(1024)S(1)} %broadcast_multiply_fusion.5), kind=kOutput, calls=%fused_computation.128 | convolution fusion | flops 8595177472 | bytes 29376512 | tf_op jit(solution)/shard_map/dot_general | solution.py:13
  369.2 51.3 %fusion.140 = (f32[1024]{0:T(1024)S(1)}, f32[1024,1024]{0,1:T(8,128)}) fusion(f32[1024]{0:T(1024)S(1)} %copy-done.47, bf16[4096,1024]{1,0:T(8,128)(2,1)} %all-gather.17.cloned.1.call-done, f32[1024,4096]{1,0:T(8,128)} %fusion.90, f32[4096]{0:T(1024)S(1)} %copy-done.40, f32[1024]{0:T(1024)S(1)} %bitcast.166, f32[1024]{0:T(1024)S(1)} %bitcast.157, ...), kind=kOutput, calls=%fused_computation.192 | convolution fusion | flops 8874097664 | bytes 33595392 | tf_op jit(solution)/shard_map/dot_general | solution.py:13
  420.6 2.8 multiply_reduce_fusion.3
  425.0 22.0 %convert_reduce_fusion = (f32[4096]{0:T(1024)}, bf16[1024,4096]{1,0:T(8,128)(2,1)}) fusion(f32[1024,4096]{1,0:T(8,128)} %fusion.90, f32[4096]{0:T(1024)S(1)} %copy-done.40, bf16[4096,1024]{1,0:T(8,128)(2,1)} %all-gather.17.cloned.1.call-done, f32[1024]{0:T(1024)S(1)} %get-tuple-element.250, f32[1024]{0:T(1024)S(1)} %add_rsqrt_fusion, ...), kind=kOutput, calls=%fused_computation.70 | convolution fusion | flops 8653893632 | bytes 39899136 | tf_op jit(solution)/shard_map/dot_general | solution.py:17
  447.1 17.5 %multiply_reduce_fusion.1 = (f32[1024]{0:T(1024)}, f32[1024]{0:T(1024)S(1)}, f32[1024]{0:T(1024)S(1)}, f32[1024]{0:T(1024)}, f32[1024,1024]{0,1:T(8,128)S(1)}) fusion(f32[1024,1024]{0,1:T(8,128)} %copy-done.11, f32[1024]{0:T(1024)S(1)} %add_rsqrt_fusion.1, f32[1024]{0:T(1024)S(1)} %broadcast_multiply_fusion.5, f32[1024]{0:T(1024)S(1)} %bitcast.158, ...), kind=kOutput, calls=%fused_computation.107 | convolution fusion | flops 8608804864 | bytes 31506432 | tf_op jit(solution)/shard_map/dot_general | solution.py:17
  464.7 2.0 convert_reduce_fusion.3
  466.7 2.1 copy-done.17
  468.7 2.4 convolution_convert_fusion
  471.1 4.0 reshape.139
  475.1 5.4 copy.90
  485.2 93.9 %while.27 = (s32[]{:T(128)}, bf16[2,512,16,64]{1,3,2,0:T(8,128)(2,1)}, bf16[2,512,16,64]{1,3,2,0:T(8,128)(2,1)}, bf16[2,512,16,64]{1,3,2,0:T(8,128)(2,1)}, bf16[...) while((s32[]{:T(128)}, ...), condition=%wide.region_14.15_spmd, body=%wide.region_12.14_spmd.sunk | while | flops 2724716544 | bytes 195205968 | solution.py:196
  485.3 9.6 %subtract_exponential_fusion.2 = f32[16,512,512]{1,2,0:T(8,128)} fusion(f32[16,512]{1,0:T(8,128)S(1)} %dynamic-slice_bitcast_fusion.2, pred[512]{0:T(512)(128)(4,1)S(1)} %dynamic-slice_reduce_fusion.5, bf16[2,512,16,64]{1,3,2,0:T(8,128)(2,1)} %get-tuple-element.420, s32[]{:T(128)} %get-tuple-element.403, ...), kind=kOutput, calls=%fused_computation.25.clone.1 | convolution fusion | flops 549453824 | bytes 18908672 | tf_op jit(solution)/shard_map/while/body/eval_jaxpr/qhd,khd->hqk/dot_general | solution.py:48
  494.9 10.5 %multiply_reduce_fusion.7 = (f32[16,512]{1,0:T(8,128)S(1)}, f32[16,512,512]{1,2,0:T(8,128)}) fusion(f32[16,512,512]{1,2,0:T(8,128)} %subtract_exponential_fusion.2, bf16[2,512,16,64]{1,3,2,0:T(8,128)(2,1)S(1)} %copy-done.6, s32[]{:T(128)} %get-tuple-element.403, bf16[2,512,16,64]{1,3,2,0:T(8,128)(2,1)S(1)} %copy-done.2), kind=kOutput, calls=%fused_computation.24.clone.1 | convolution fusion | flops 545251328 | bytes 35685376 | tf_op jit(solution)/shard_map/while/body/eval_jaxpr/qhd,khd->hqk/dot_general | solution.py:73
  505.4 11.9 %multiply_convert_fusion.4 = bf16[16,512,512]{1,2,0:T(8,128)(2,1)S(1)} fusion(f32[16,512,512]{1,2,0:T(8,128)} %subtract_exponential_fusion.2, f32[16,512,512]{1,2,0:T(8,128)} %get-tuple-element.366, f32[16,512]{1,0:T(8,128)S(1)} %get-tuple-element.367), kind=kLoop, calls=%fused_computation.23.clone.1 | loop fusion | flops 12582912 | bytes 41975808 | tf_op jit(solution)/shard_map/while/body/eval_jaxpr/convert_element_type | solution.py:81
  517.3 2.6 fusion.180
  522.8 9.4 %fusion.181 = bf16[2,512,16,64]{1,3,2,0:T(8,128)(2,1)} fusion(bf16[2,512,16,64]{1,3,2,0:T(8,128)(2,1)} %get-tuple-element.406, s32[]{:T(128)} %get-tuple-element.403, f32[16,512,512]{1,2,0:T(8,128)} %subtract_exponential_fusion.2, bf16[2,512,16,64]{1,3,2,0:T(8,128)(2,1)S(1)} %copy-done.2), kind=kOutput, calls=%fused_computation.36.clone.1 | convolution fusion | flops 541589504 | bytes 18875392 | tf_op jit(solution)/shard_map/while/body/eval_jaxpr/hqk,qhd->khd/dot_general | solution.py:74
  532.2 9.6 %subtract_exponential_fusion.2 = f32[16,512,512]{1,2,0:T(8,128)} fusion(f32[16,512]{1,0:T(8,128)S(1)} %dynamic-slice_bitcast_fusion.2, pred[512]{0:T(512)(128)(4,1)S(1)} %dynamic-slice_reduce_fusion.5, bf16[2,512,16,64]{1,3,2,0:T(8,128)(2,1)} %get-tuple-element.420, s32[]{:T(128)} %get-tuple-element.403, ...), kind=kOutput, calls=%fused_computation.25.clone.1 | convolution fusion | flops 549453824 | bytes 18908672 | tf_op jit(solution)/shard_map/while/body/eval_jaxpr/qhd,khd->hqk/dot_general | solution.py:48
  541.9 10.5 %multiply_reduce_fusion.7 = (f32[16,512]{1,0:T(8,128)S(1)}, f32[16,512,512]{1,2,0:T(8,128)}) fusion(f32[16,512,512]{1,2,0:T(8,128)} %subtract_exponential_fusion.2, bf16[2,512,16,64]{1,3,2,0:T(8,128)(2,1)S(1)} %copy-done.6, s32[]{:T(128)} %get-tuple-element.403, bf16[2,512,16,64]{1,3,2,0:T(8,128)(2,1)S(1)} %copy-done.2), kind=kOutput, calls=%fused_computation.24.clone.1 | convolution fusion | flops 545251328 | bytes 35685376 | tf_op jit(solution)/shard_map/while/body/eval_jaxpr/qhd,khd->hqk/dot_general | solution.py:73
  552.3 11.9 %multiply_convert_fusion.4 = bf16[16,512,512]{1,2,0:T(8,128)(2,1)S(1)} fusion(f32[16,512,512]{1,2,0:T(8,128)} %subtract_exponential_fusion.2, f32[16,512,512]{1,2,0:T(8,128)} %get-tuple-element.366, f32[16,512]{1,0:T(8,128)S(1)} %get-tuple-element.367), kind=kLoop, calls=%fused_computation.23.clone.1 | loop fusion | flops 12582912 | bytes 41975808 | tf_op jit(solution)/shard_map/while/body/eval_jaxpr/convert_element_type | solution.py:81
  564.2 2.6 fusion.180
  569.7 9.4 %fusion.181 = bf16[2,512,16,64]{1,3,2,0:T(8,128)(2,1)} fusion(bf16[2,512,16,64]{1,3,2,0:T(8,128)(2,1)} %get-tuple-element.406, s32[]{:T(128)} %get-tuple-element.403, f32[16,512,512]{1,2,0:T(8,128)} %subtract_exponential_fusion.2, bf16[2,512,16,64]{1,3,2,0:T(8,128)(2,1)S(1)} %copy-done.2), kind=kOutput, calls=%fused_computation.36.clone.1 | convolution fusion | flops 541589504 | bytes 18875392 | tf_op jit(solution)/shard_map/while/body/eval_jaxpr/hqk,qhd->khd/dot_general | solution.py:74
  579.1 1.9 convert_reduce_fusion.5
  581.1 6.2 copy.112
  587.3 2.1 convert_reduce_fusion.4
  589.4 6.2 copy.114
  595.6 5.5 fusion.82
  601.3 6.6 reshape.140
  607.9 4.8 copy.113
  612.6 6.5 reshape.141
  619.2 6.6 reshape.142
  625.8 12.7 %fusion.83 = bf16[1024,1024]{0,1:T(8,128)(2,1)} fusion(f32[1024,1024]{0,1:T(8,128)} %copy-done.17, bf16[3,1024,1024]{2,1,0:T(8,128)(2,1)} %reshape.133, bf16[1,1024,1024]{2,1,0:T(8,128)(2,1)} %reshape.142, bf16[1,1024,1024]{2,1,0:T(8,128)(2,1)} %reshape.141, bf16[1,1024,1024]{2,1,0:T(8,128)(2,1)S(1)} %copy-done.18), kind=kOutput, calls=%fused_computation.106 | convolution fusion | flops 6450839552 | bytes 18874368 | tf_op jit(solution)/shard_map/mte,mde->td/dot_general | solution.py:206
  638.5 4.1 copy.100
  642.6 2.5 copy.99
  645.2 40.6 %all-reduce = (f32[3,1024]{1,0:T(4,128)}, f32[4096]{0:T(1024)}, f32[1024]{0:T(1024)}, f32[2,1024]{1,0:T(2,128)}, f32[2,1024]{1,0:T(2,128)}) all-reduce(f32[3,1024]{1,0:T(4,128)S(1)} %pad_maximum_fusion, f32[4096]{0:T(1024)S(1)} %copy-done.41, f32[1024]{0:T(1024)S(1)} %get-tuple-element.179, ...), channel_id=1, replica_groups=mesh['dp'=8,'tensor'=4] {'dp','tensor'}, use_global_device_ids=true, to_apply=%region_18.19 | all-reduce | flops 12288 | bytes 98304 | tf_op jit(solution)/shard_map/psum | solution.py:213
  (176 shorter events, 22.3 us)
Async XLA Ops:
  7.2 56.3 %copy-start.19 = (bf16[1024,1024]{1,0:T(8,128)(2,1)S(1)}, bf16[1024,1024]{1,0:T(8,128)(2,1)}, u32[]{:S(2)}) copy-start(bf16[1024,1024]{1,0:T(8,128)(2,1)} %param.18) | copy-start | bytes 6291460
  7.2 58.9 %copy-start.46 = (s32[2,512]{1,0:T(2,128)S(1)}, s32[2,512]{1,0:T(2,128)}, u32[]{:S(2)}) copy-start(s32[2,512]{1,0:T(2,128)} %param.19) | copy-start | bytes 12292
  7.2 59.1 %copy-start.45 = (bf16[4096]{0:T(1024)(128)(2,1)S(1)}, bf16[4096]{0:T(1024)(128)(2,1)}, u32[]{:S(2)}) copy-start(bf16[4096]{0:T(1024)(128)(2,1)} %param.27) | copy-start | bytes 24580
  7.2 59.7 %copy-start.50 = (bf16[1024]{0:T(1024)(128)(2,1)S(1)}, bf16[1024]{0:T(1024)(128)(2,1)}, u32[]{:S(2)}) copy-start(bf16[1024]{0:T(1024)(128)(2,1)} %param.28) | copy-start | bytes 6148
  7.2 54.8 %all-gather.11.cloned.1.call-start = ((), (), s32[]{:S(2)}) async-start(), calls=%async_computation.2 | async-start | bytes 2359296 | tf_op jit(solution)/shard_map/all_gather | solution.py:128
  7.9 105.0 %all-gather.15.cloned.1.call-start = ((), (), s32[]{:S(2)}) async-start(), calls=%async_computation.4 | async-start | bytes 2359296 | tf_op jit(solution)/shard_map/all_gather | solution.py:129
  8.7 161.5 %all-gather.9.cloned.1.call-start = ((), (), s32[]{:S(2)}) async-start(), calls=%async_computation.1 | async-start | bytes 2162688 | tf_op jit(solution)/shard_map/all_gather | solution.py:123
  9.4 231.6 %all-gather.7.cloned.1.call-start = ((), (), s32[]{:S(2)}) async-start(), calls=%async_computation | async-start | bytes 6488064 | tf_op jit(solution)/shard_map/all_gather | solution.py:122
  10.0 342.3 %all-gather.13.cloned.1.call-start = ((), (), s32[]{:S(2)}) async-start(), calls=%async_computation.3 | async-start | bytes 10485760 | tf_op jit(solution)/shard_map/all_gather | solution.py:132
  62.0 307.2 %all-gather.17.cloned.1.call-start = ((), (), s32[]{:S(2)}) async-start(), calls=%async_computation.5 | async-start | bytes 10485760 | tf_op jit(solution)/shard_map/all_gather | solution.py:133
  63.5 8.0 %copy-start.51 = (s32[2]{0:T(128)S(1)}, s32[2]{0:T(128)}, u32[]{:S(2)}) copy-start(s32[2]{0:T(128)} %param.20) | copy-start | bytes 28
  63.5 8.0 %copy-start.42 = (bf16[2,1024]{1,0:T(2,128)(2,1)S(1)}, bf16[2,1024]{1,0:T(2,128)(2,1)}, u32[]{:S(2)}) copy-start(bf16[2,1024]{1,0:T(2,128)(2,1)} %param.21) | copy-start | bytes 12292
  63.5 8.0 %copy-start.43 = (bf16[2,1024]{1,0:T(2,128)(2,1)S(1)}, bf16[2,1024]{1,0:T(2,128)(2,1)}, u32[]{:S(2)}) copy-start(bf16[2,1024]{1,0:T(2,128)(2,1)} %param.29) | copy-start | bytes 12292
  63.5 8.6 %copy-start.44 = (bf16[2,1024]{1,0:T(2,128)(2,1)S(1)}, bf16[2,1024]{1,0:T(2,128)(2,1)}, u32[]{:S(2)}) copy-start(bf16[2,1024]{1,0:T(2,128)(2,1)} %param.30) | copy-start | bytes 12292
  174.4 77.2 %copy-start.22 = (bf16[1024,1024]{0,1:T(8,128)(2,1)S(1)}, bf16[1024,1024]{0,1:T(8,128)(2,1)}, u32[]{:S(2)}) copy-start(bf16[1024,1024]{0,1:T(8,128)(2,1)} %copy.75) | copy-start | bytes 6291460
  318.8 3.9 copy-start.5
  332.5 3.9 copy-start.5
  341.7 5.2 copy-start
  341.7 5.2 copy-start.24
  341.7 5.2 copy-start.26
  341.7 5.2 copy-start.20
  341.7 5.2 copy-start.23
  349.9 2.0 copy-start.11
  352.3 16.9 %copy-start.40 = (f32[4096]{0:T(1024)S(1)}, f32[4096]{0:T(1024)}, u32[]{:S(2)}) copy-start(f32[4096]{0:T(1024)} %convert_element_type.124) | copy-start | bytes 49156
  352.3 16.9 %copy-start.47 = (f32[1024]{0:T(1024)S(1)}, f32[1024]{0:T(1024)}, u32[]{:S(2)}) copy-start(f32[1024]{0:T(1024)} %convert_element_type.126) | copy-start | bytes 12292
  369.2 54.2 %copy-start.9 = (bf16[1024,1024]{0,1:T(8,128)(2,1)S(1)}, bf16[1024,1024]{0,1:T(8,128)(2,1)}, u32[]{:S(2)}) copy-start(bf16[1024,1024]{0,1:T(8,128)(2,1)} %copy.85) | copy-start | bytes 6291460
  420.5 3.5 copy-start.4
  420.5 3.4 copy-start.32
  420.6 26.5 %copy-start.28 = (f32[1024]{0:T(1024)}, f32[1024]{0:T(1024)S(1)}, u32[]{:S(2)}) copy-start(f32[1024]{0:T(1024)S(1)} %broadcast_multiply_fusion.4) | copy-start | bytes 12292
  423.4 23.7 %copy-start.30 = (f32[1024]{0:T(1024)}, f32[1024]{0:T(1024)S(1)}, u32[]{:S(2)}) copy-start(f32[1024]{0:T(1024)S(1)} %add_rsqrt_fusion) | copy-start | bytes 12292
  425.0 22.1 %copy-start.36 = (f32[1024]{0:T(1024)}, f32[1024]{0:T(1024)S(1)}, u32[]{:S(2)}) copy-start(f32[1024]{0:T(1024)S(1)} %get-tuple-element.250) | copy-start | bytes 12292
  425.0 22.1 %copy-start.38 = (f32[1024]{0:T(1024)}, f32[1024]{0:T(1024)S(1)}, u32[]{:S(2)}) copy-start(f32[1024]{0:T(1024)S(1)} %get-tuple-element.251) | copy-start | bytes 12292
  447.1 17.5 %copy-start.12 = (f32[1024,1024]{0,1:T(8,128)S(1)}, f32[1024,1024]{0,1:T(8,128)}, u32[]{:S(2)}) copy-start(f32[1024,1024]{0,1:T(8,128)} %copy-done.11) | copy-start | bytes 12582916
  464.6 4.1 copy-start.21
  466.7 2.1 copy-start.17
  480.6 4.7 copy-start.1
  480.6 4.7 copy-start.25
  480.6 4.7 copy-start.27
  485.3 9.7 %copy-start.2 = (bf16[2,512,16,64]{1,3,2,0:T(8,128)(2,1)S(1)}, bf16[2,512,16,64]{1,3,2,0:T(8,128)(2,1)}, u32[]{:S(2)}) copy-start(bf16[2,512,16,64]{1,3,2,0:T(8,128)(2,1)} %get-tuple-element.422) | copy-start | bytes 6291460 | tf_op jit(solution)/shard_map/while
  485.3 9.6 %copy-start.6 = (bf16[2,512,16,64]{1,3,2,0:T(8,128)(2,1)S(1)}, bf16[2,512,16,64]{1,3,2,0:T(8,128)(2,1)}, u32[]{:S(2)}) copy-start(bf16[2,512,16,64]{1,3,2,0:T(8,128)(2,1)} %get-tuple-element.423) | copy-start | bytes 6291460 | tf_op jit(solution)/shard_map/while
  505.4 11.9 %copy-start.3 = (bf16[2,512,16,64]{1,3,2,0:T(8,128)(2,1)S(1)}, bf16[2,512,16,64]{1,3,2,0:T(8,128)(2,1)}, u32[]{:S(2)}) copy-start(bf16[2,512,16,64]{1,3,2,0:T(8,128)(2,1)} %get-tuple-element.420) | copy-start | bytes 6291460 | tf_op jit(solution)/shard_map/while
  505.4 11.9 %copy-start.13 = (bf16[2,512,16,64]{1,3,2,0:T(8,128)(2,1)S(1)}, bf16[2,512,16,64]{1,3,2,0:T(8,128)(2,1)}, u32[]{:S(2)}) copy-start(bf16[2,512,16,64]{1,3,2,0:T(8,128)(2,1)} %get-tuple-element.405) | copy-start | bytes 6291460 | tf_op jit(solution)/shard_map/while
  517.3 2.7 copy-start.7
  519.9 1.5 copy-start.14
  532.2 9.6 %copy-start.2 = (bf16[2,512,16,64]{1,3,2,0:T(8,128)(2,1)S(1)}, bf16[2,512,16,64]{1,3,2,0:T(8,128)(2,1)}, u32[]{:S(2)}) copy-start(bf16[2,512,16,64]{1,3,2,0:T(8,128)(2,1)} %get-tuple-element.422) | copy-start | bytes 6291460 | tf_op jit(solution)/shard_map/while
  532.2 9.6 %copy-start.6 = (bf16[2,512,16,64]{1,3,2,0:T(8,128)(2,1)S(1)}, bf16[2,512,16,64]{1,3,2,0:T(8,128)(2,1)}, u32[]{:S(2)}) copy-start(bf16[2,512,16,64]{1,3,2,0:T(8,128)(2,1)} %get-tuple-element.423) | copy-start | bytes 6291460 | tf_op jit(solution)/shard_map/while
  552.3 11.9 %copy-start.3 = (bf16[2,512,16,64]{1,3,2,0:T(8,128)(2,1)S(1)}, bf16[2,512,16,64]{1,3,2,0:T(8,128)(2,1)}, u32[]{:S(2)}) copy-start(bf16[2,512,16,64]{1,3,2,0:T(8,128)(2,1)} %get-tuple-element.420) | copy-start | bytes 6291460 | tf_op jit(solution)/shard_map/while
  552.3 11.9 %copy-start.13 = (bf16[2,512,16,64]{1,3,2,0:T(8,128)(2,1)S(1)}, bf16[2,512,16,64]{1,3,2,0:T(8,128)(2,1)}, u32[]{:S(2)}) copy-start(bf16[2,512,16,64]{1,3,2,0:T(8,128)(2,1)} %get-tuple-element.405) | copy-start | bytes 6291460 | tf_op jit(solution)/shard_map/while
  564.2 2.7 copy-start.7
  566.9 1.5 copy-start.14
  587.2 8.3 %copy-start.10 = (bf16[1024,1024]{0,1:T(8,128)(2,1)S(1)}, bf16[1024,1024]{0,1:T(8,128)(2,1)}, u32[]{:S(2)}) copy-start(bf16[1024,1024]{0,1:T(8,128)(2,1)} %copy.85) | copy-start | bytes 6291460
  587.2 8.3 %copy-start.29 = (f32[1024]{0:T(1024)S(1)}, f32[1024]{0:T(1024)}, u32[]{:S(2)}) copy-start(f32[1024]{0:T(1024)} %copy-done.28) | copy-start | bytes 12292
  587.3 8.3 %copy-start.31 = (f32[1024]{0:T(1024)S(1)}, f32[1024]{0:T(1024)}, u32[]{:S(2)}) copy-start(f32[1024]{0:T(1024)} %copy-done.30) | copy-start | bytes 12292
  587.3 8.3 %copy-start.33 = (f32[1,1024]{1,0:T(1,128)S(1)}, f32[1,1024]{1,0:T(1,128)}, u32[]{:S(2)}) copy-start(f32[1,1024]{1,0:T(1,128)} %get-tuple-element.237) | copy-start | bytes 12292
  587.3 8.4 %copy-start.35 = (f32[1,1024]{1,0:T(1,128)S(1)}, f32[1,1024]{1,0:T(1,128)}, u32[]{:S(2)}) copy-start(f32[1,1024]{1,0:T(1,128)} %get-tuple-element.239) | copy-start | bytes 12292
  587.3 8.3 %copy-start.37 = (f32[1024]{0:T(1024)S(1)}, f32[1024]{0:T(1024)}, u32[]{:S(2)}) copy-start(f32[1024]{0:T(1024)} %copy-done.36) | copy-start | bytes 12292
  587.3 8.3 %copy-start.39 = (f32[1024]{0:T(1024)S(1)}, f32[1024]{0:T(1024)}, u32[]{:S(2)}) copy-start(f32[1024]{0:T(1024)} %copy-done.38) | copy-start | bytes 12292
  601.1 6.8 copy-start.15
  619.2 6.6 copy-start.18
  638.5 4.1 copy-start.16
  638.5 6.7 copy-start.49
  638.5 6.7 copy-start.48
  638.5 6.7 copy-start.34
  638.5 6.7 copy-start.41
  (2 other events, 2.6 us)
Sparse Core Ops, SparseCore 0:
  10.1 51.7 all-gather.10
  64.0 48.8 all-gather.14
  115.8 54.3 all-gather.8
  172.9 67.9 all-gather.6
  242.4 56.7 all-gather.12
  300.6 58.2 all-gather.16
where the time goes:
time: 704 us; the launch traced here: 693 us
  matrix products  224 us (32%)
  waiting for transfers between devices  219 us (31%)
  local copies, waits for them, and re-layouts  136 us (19%)
  other arithmetic  57.2 us (8%)
  blocking collectives  40.6 us (6%)
  between operations  15.1 us (2%)
    dot_general x3, matrix products, matmul(): return jnp.dot(left_side, right_side, preferred_element_type=jnp.float32)  71.1 us
    all_gather x1, waiting for transfers between devices, per_device(): lax.all_gather(attn_weight, ('dp', 'tensor'), axis=0, tiled=True)  66.6 us
    all_gather x1, waiting for transfers between devices, per_device(): lax.all_gather(out_weight, ('dp', 'tensor'), axis=0, tiled=True)  57.3 us
    all_gather x1, waiting for transfers between devices, per_device(): lax.all_gather(ffn_in_weight, 'dp', axis=0, tiled=True)  51.9 us
    dot_general x3, matrix products, matmul_t(): lax.dot_general(left_side, right_side, (((1,), (1,)), ((), ())), preferre...  42 us
    psum x1, blocking collectives, per_device(): lax.psum((attn_grad, bias_in_grad, bias_out_grad, gain_grad, shift_grad),...  40.6 us
    all_gather x1, waiting for transfers between devices, per_device(): lax.all_gather(ffn_out_weight, 'dp', axis=1, tiled=True)  40.2 us
    another operation x6, local copies, waits for them, and re-layouts, per_device(): stacked = jnp.stack([d_queries, d_keys, d_values])  36.9 us
  transfers between devices with their start and end apart: 6, of which 4 were waited for; matrix products, arithmetic and copies ran while one was open for 20% of the time, Pallas kernels for 0%

commit v1 on v0

--- a/solution.py
+++ b/solution.py
@@ -1,3 +1,4 @@
+import functools
 from functools import partial
 import math
 import jax
@@ -7,6 +8,40 @@
 
 HEADS = 16
 HEAD = 64
+
+
+def groups_step_on(block_here, dim_k):
+    later = list(block_here.shape[1:])
+    later[dim_k] *= block_here.shape[0]
+    w2 = jnp.moveaxis(block_here, 0, dim_k).reshape(later)
+    return w2
+
+
+def do_the_regions(field, row_axis, ndim_at):
+    inbox = []
+    num = lax.axis_size(row_axis)
+    for kk in range(num):
+        inbox.append((kk, (kk + 1) % num))
+    grid = []
+    for ix, k in inbox:
+        grid.append((k, ix))
+    k_now, u1 = ([], [])
+    for dev_j in range(num - 1):
+        if dev_j % 2 == 0:
+            opened = lax.ppermute(k_now[-1] if k_now else field, row_axis, inbox)
+            k_now.append(opened)
+        else:
+            p_next = lax.ppermute(u1[-1] if u1 else field, row_axis, grid)
+            u1.append(p_next)
+    y = jnp.stack([*k_now[::-1], field, *u1])
+    current_value = lax.axis_index(row_axis)
+    item_now = current_value - len(k_now)
+    y = y[(jnp.arange(num) - item_now) % num]
+    heard = groups_step_on(y, ndim_at)
+    return heard
+
+
+press_page = functools.partial(do_the_regions, row_axis="dp", ndim_at=0)
 
 
 def matmul(left_side, right_side):
@@ -125,7 +160,7 @@
     projections = qkv_flat.reshape(3, model_width, model_width)
     out_proj = out_flat.reshape(model_width, model_width)
     w_first, w_second = (
-        lax.all_gather(ffn_in_weight, "dp", axis=0, tiled=True),
+        press_page(ffn_in_weight),
         lax.all_gather(ffn_out_weight, "dp", axis=1, tiled=True),
     )
     w_first, w_second = (

time: 704 us -> 728 us (1.034)
  starting transfers between devices: 0.23 us -> 15.2 us
    ppermute x0 -> x7, waiting for transfers between devices: none -> 42 us  [the longest x4 39.5 us: do_the_regions(): opened = lax.ppermute(k_now[-1] if k_now else field, row_axis, inbox)]
    all_gather x1, waiting for transfers between devices: 40.2 us -> 10.4 us  [per_device(): lax.all_gather(ffn_out_weight, 'dp', axis=1, tiled=True)]
    ppermute x0 -> x7, starting transfers between devices: none -> 15 us  [the longest x3 8.03 us: do_the_regions(): p_next = lax.ppermute(u1[-1] if u1 else field, row_axis, grid)]
    all_gather x1, waiting for transfers between devices: 51.9 us -> 41.6 us  [per_device(): lax.all_gather(ffn_in_weight, 'dp', axis=0, tiled=True)]
    unnamed x93 -> x102, local copies, waits for them, and re-layouts: 18.4 us -> 20.6 us
  transfers between devices with their start and end apart: 6 -> 14, of which waited for: 4 -> 9; matrix products, arithmetic and copies ran while one was open for 20% -> 31% of each run, Pallas kernels for 0% -> 0%
where the time goes in v1:
time: 728 us; the launch traced here: 717 us
  matrix products  228 us (31%)
  waiting for transfers between devices  221 us (30%)
  local copies, waits for them, and re-layouts  140 us (19%)
  other arithmetic  56.5 us (8%)
  blocking collectives  40.5 us (6%)
  starting transfers between devices  15.2 us (2%)
  between operations  15.2 us (2%)
    dot_general x3, matrix products, matmul(): return jnp.dot(left_side, right_side, preferred_element_type=jnp.float32)  73.2 us
    all_gather x1, waiting for transfers between devices, per_device(): lax.all_gather(attn_weight, ('dp', 'tensor'), axis=0, tiled=True)  66.6 us
    all_gather x1, waiting for transfers between devices, per_device(): lax.all_gather(out_weight, ('dp', 'tensor'), axis=0, tiled=True)  57.6 us
    dot_general x3, matrix products, matmul_t(): lax.dot_general(left_side, right_side, (((1,), (1,)), ((), ())), preferre...  43 us
    all_gather x1, waiting for transfers between devices, per_device(): lax.all_gather(ffn_in_weight, 'dp', axis=0, tiled=True)  41.6 us
    psum x1, blocking collectives, per_device(): lax.psum((attn_grad, bias_in_grad, bias_out_grad, gain_grad, shift_grad),...  40.5 us
    ppermute x4, waiting for transfers between devices, do_the_regions(): opened = lax.ppermute(k_now[-1] if k_now else field, row_axis, inbox)  39.5 us
    another operation x6, local copies, waits for them, and re-layouts, per_device(): stacked = jnp.stack([d_queries, d_keys, d_values])  36.9 us
  transfers between devices with their start and end apart: 14, of which 9 were waited for; matrix products, arithmetic and copies ran while one was open for 31% of the time, Pallas kernels for 0%

profile of v1, /device:TPU:0, one launch (start us, length us, event | category | flops | bytes accessed | tf_op | source)
XLA Modules:
  0.0 716.9 jit_solution(17740626177619197799)
XLA Ops:
  10.0 3.0 collective-permute-start
  13.1 9.6 %collective-permute-done = bf16[128,1024]{1,0:T(8,128)(2,1)S(1)} collective-permute-done((bf16[128,1024]{1,0:T(8,128)(2,1)}, bf16[128,1024]{1,0:T(8,128)(2,1)S(1)}, u32[]{:S(2)}, u32[]{:S(2)}) %collective-permute-start) | collective-permute-done | bytes 262176 | tf_op jit(solution)/shard_map/ppermute | solution.py:31
  22.6 4.7 collective-permute-start.4
  27.3 9.0 %collective-permute-done.1 = bf16[128,1024]{1,0:T(8,128)(2,1)S(1)} collective-permute-done((bf16[128,1024]{1,0:T(8,128)(2,1)S(1)}, bf16[128,1024]{1,0:T(8,128)(2,1)S(1)}, u32[]{:S(2)}, u32[]{:S(2)}) %collective-permute-start.1) | collective-permute-done | bytes 262176 | tf_op jit(solution)/shard_map/ppermute | solution.py:31
  37.8 3.3 collective-permute-start.5
  41.1 7.6 %collective-permute-done.2 = bf16[128,1024]{1,0:T(8,128)(2,1)S(1)} collective-permute-done((bf16[128,1024]{1,0:T(8,128)(2,1)S(1)}, bf16[128,1024]{1,0:T(8,128)(2,1)S(1)}, u32[]{:S(2)}, u32[]{:S(2)}) %collective-permute-start.2) | collective-permute-done | bytes 262176 | tf_op jit(solution)/shard_map/ppermute | solution.py:31
  51.3 2.5 collective-permute-done.5
  53.8 13.3 %collective-permute-done.3 = bf16[128,1024]{1,0:T(8,128)(2,1)} collective-permute-done((bf16[128,1024]{1,0:T(8,128)(2,1)S(1)}, bf16[128,1024]{1,0:T(8,128)(2,1)}, u32[]{:S(2)}, u32[]{:S(2)}) %collective-permute-start.3) | collective-permute-done | bytes 262176 | tf_op jit(solution)/shard_map/ppermute | solution.py:31
  71.3 10.4 %all-gather.14.cloned.1.call-done = bf16[1024,1024]{1,0:T(8,128)(2,1)} async-done(((bf16[1024,128]{1,0:T(8,128)(2,1)}), bf16[1024,1024]{1,0:T(8,128)(2,1)}) %all-gather.14.cloned.1.call-update) | async-done | bytes 2097168 | tf_op jit(solution)/shard_map/all_gather | solution.py:164
  81.9 2.7 copy.75
  85.9 3.9 copy.85
  91.2 41.6 %all-gather.18.cloned.1.call-done = bf16[1024,1024]{1,0:T(8,128)(2,1)} async-done(((bf16[128,1024]{1,0:T(8,128)(2,1)}), bf16[1024,1024]{1,0:T(8,128)(2,1)}) %all-gather.18.cloned.1.call-update) | async-done | bytes 2097168 | tf_op jit(solution)/shard_map/all_gather | solution.py:209
  132.8 57.6 %all-gather.10.cloned.1.call-done = bf16[1048576]{0:T(1024)(128)(2,1)} async-done(((bf16[32768]{0:T(1024)(128)(2,1)}), bf16[1048576]{0:T(1024)(128)(2,1)}) %all-gather.10.cloned.1.call-update) | async-done | bytes 2097168 | tf_op jit(solution)/shard_map/all_gather | solution.py:158
  190.4 4.2 reshape.187
  194.5 66.6 %all-gather.8.cloned.1.call-done = bf16[3145728]{0:T(1024)(128)(2,1)} async-done(((bf16[98304]{0:T(1024)(128)(2,1)}), bf16[3145728]{0:T(1024)(128)(2,1)}) %all-gather.8.cloned.1.call-update) | async-done | bytes 6291472 | tf_op jit(solution)/shard_map/all_gather | solution.py:157
  261.1 10.5 %reshape.185 = bf16[3,1024,1024]{2,1,0:T(8,128)(2,1)} reshape(bf16[3145728]{0:T(1024)(128)(2,1)} %all-gather.8.cloned.1.call-done) | data formatting | bytes 12582912 | tf_op jit(solution)/shard_map/reshape | solution.py:160
  271.7 12.1 %convolution_bitcast_fusion = f32[3,1024,1024]{2,1,0:T(8,128)S(1)} fusion(bf16[3,1024,1024]{2,1,0:T(8,128)(2,1)} %reshape.185, bf16[1024,1024]{0,1:T(8,128)(2,1)S(1)} %copy-done.22, f32[1024]{0:T(1024)S(1)} %bitcast.189, f32[1024]{0:T(1024)S(1)} %bitcast.187, pred[1024]{0:T(1024)(128)(4,1)S(1)} %eq.17), kind=kOutput, calls=%fused_computation.100 | convolution fusion | flops 6446645248 | bytes 20980736 | tf_op jit(solution)/shard_map/td,mde->mte/dot_general | solution.py:176
  283.8 4.2 fusion.137
  288.3 5.4 copy.77
  293.7 6.7 squeeze.34
  300.4 3.9 add_convert_fusion.2
  306.1 5.5 copy.78
  311.6 6.6 squeeze.35
  318.1 3.9 add_convert_fusion.1
  323.9 3.9 reshape.204
  327.8 4.9 copy.82
  334.3 28.1 %while.26 = (s32[]{:T(128)}, bf16[2,512,16,64]{1,3,2,0:T(8,128)(2,1)}, f32[2,16,512,1]{2,1,3,0:T(8,128)S(1)}, bf16[2,512,16,64]{1,3,2,0:T(8,128)(2,1)}, pred[2,5...) while((s32[]{:T(128)}, ...), condition=%wide.region_3.4_spmd, body=%wide.region_0.3_spmd.sunk | while | flops 1120395264 | bytes 63181432 | solution.py:185
  334.4 5.1 fusion.171
  339.4 3.8 exponential_reduce_fusion.2
  343.3 4.9 fusion.172
  348.2 5.1 fusion.171
  353.3 3.8 exponential_reduce_fusion.2
  357.2 4.8 fusion.172
  362.5 4.6 copy.83
  367.6 3.0 fusion.141
  373.1 17.7 %fusion.90 = f32[1024,4096]{1,0:T(8,128)} fusion(bf16[1024,4096]{1,0:T(8,128)(2,1)} %all-gather.12.cloned.1.call-done, f32[1024,1024]{0,1:T(8,128)} %copy-done.11, f32[1024]{0:T(1024)S(1)} %bitcast.185, f32[1024]{0:T(1024)S(1)} %bitcast.176, f32[1024]{0:T(1024)S(1)} %add_rsqrt_fusion.1, f32[1024]{0:T(1024)S(1)} %broadcast_multiply_fusion.5), kind=kOutput, calls=%fused_computation.129 | convolution fusion | flops 8595177472 | bytes 29376512 | tf_op jit(solution)/shard_map/dot_general | solution.py:48
  390.8 52.6 %fusion.142 = (f32[1024]{0:T(1024)S(1)}, f32[1024,1024]{0,1:T(8,128)}) fusion(f32[1024]{0:T(1024)S(1)} %copy-done.48, bf16[4096,1024]{1,0:T(8,128)(2,1)} %all-gather.16.cloned.1.call-done, f32[1024,4096]{1,0:T(8,128)} %fusion.90, f32[4096]{0:T(1024)S(1)} %copy-done.41, f32[1024]{0:T(1024)S(1)} %bitcast.186, f32[1024]{0:T(1024)S(1)} %bitcast.177, ...), kind=kOutput, calls=%fused_computation.208 | convolution fusion | flops 8874097664 | bytes 33595392 | tf_op jit(solution)/shard_map/dot_general | solution.py:48
  443.5 2.8 multiply_reduce_fusion.3
  448.0 21.9 %convert_reduce_fusion = (f32[4096]{0:T(1024)}, bf16[1024,4096]{1,0:T(8,128)(2,1)}) fusion(f32[1024,4096]{1,0:T(8,128)} %fusion.90, f32[4096]{0:T(1024)S(1)} %copy-done.41, bf16[4096,1024]{1,0:T(8,128)(2,1)} %all-gather.16.cloned.1.call-done, f32[1024]{0:T(1024)S(1)} %get-tuple-element.250, f32[1024]{0:T(1024)S(1)} %add_rsqrt_fusion, ...), kind=kOutput, calls=%fused_computation.71 | convolution fusion | flops 8653893632 | bytes 39899136 | tf_op jit(solution)/shard_map/dot_general | solution.py:52
  469.9 18.7 %multiply_reduce_fusion.1 = (f32[1024]{0:T(1024)}, f32[1024]{0:T(1024)S(1)}, f32[1024]{0:T(1024)S(1)}, f32[1024]{0:T(1024)}, f32[1024,1024]{0,1:T(8,128)S(1)}) fusion(f32[1024,1024]{0,1:T(8,128)} %copy-done.11, f32[1024]{0:T(1024)S(1)} %add_rsqrt_fusion.1, f32[1024]{0:T(1024)S(1)} %broadcast_multiply_fusion.5, f32[1024]{0:T(1024)S(1)} %bitcast.178, ...), kind=kOutput, calls=%fused_computation.108 | convolution fusion | flops 8608804864 | bytes 31506432 | tf_op jit(solution)/shard_map/dot_general | solution.py:52
  495.1 4.0 reshape.200
  499.1 5.5 copy.90
  509.3 93.8 %while.27 = (s32[]{:T(128)}, bf16[2,512,16,64]{1,3,2,0:T(8,128)(2,1)}, bf16[2,512,16,64]{1,3,2,0:T(8,128)(2,1)}, bf16[2,512,16,64]{1,3,2,0:T(8,128)(2,1)}, bf16[...) while((s32[]{:T(128)}, ...), condition=%wide.region_14.15_spmd, body=%wide.region_12.14_spmd.sunk | while | flops 2724716544 | bytes 195205968 | solution.py:231
  509.3 9.6 %subtract_exponential_fusion.2 = f32[16,512,512]{1,2,0:T(8,128)} fusion(f32[16,512]{1,0:T(8,128)S(1)} %dynamic-slice_bitcast_fusion.2, pred[512]{0:T(512)(128)(4,1)S(1)} %dynamic-slice_reduce_fusion.5, bf16[2,512,16,64]{1,3,2,0:T(8,128)(2,1)} %get-tuple-element.420, s32[]{:T(128)} %get-tuple-element.403, ...), kind=kOutput, calls=%fused_computation.26.clone.1 | convolution fusion | flops 549453824 | bytes 18908672 | tf_op jit(solution)/shard_map/while/body/eval_jaxpr/qhd,khd->hqk/dot_general | solution.py:83
  518.9 10.5 %multiply_reduce_fusion.7 = (f32[16,512]{1,0:T(8,128)S(1)}, f32[16,512,512]{1,2,0:T(8,128)}) fusion(f32[16,512,512]{1,2,0:T(8,128)} %subtract_exponential_fusion.2, bf16[2,512,16,64]{1,3,2,0:T(8,128)(2,1)S(1)} %copy-done.6, s32[]{:T(128)} %get-tuple-element.403, bf16[2,512,16,64]{1,3,2,0:T(8,128)(2,1)S(1)} %copy-done.2), kind=kOutput, calls=%fused_computation.25.clone.1 | convolution fusion | flops 545251328 | bytes 35685376 | tf_op jit(solution)/shard_map/while/body/eval_jaxpr/qhd,khd->hqk/dot_general | solution.py:108
  529.4 11.9 %multiply_convert_fusion.4 = bf16[16,512,512]{1,2,0:T(8,128)(2,1)S(1)} fusion(f32[16,512,512]{1,2,0:T(8,128)} %subtract_exponential_fusion.2, f32[16,512,512]{1,2,0:T(8,128)} %get-tuple-element.366, f32[16,512]{1,0:T(8,128)S(1)} %get-tuple-element.367), kind=kLoop, calls=%fused_computation.24.clone.1 | loop fusion | flops 12582912 | bytes 41975808 | tf_op jit(solution)/shard_map/while/body/eval_jaxpr/convert_element_type | solution.py:116
  541.3 2.6 fusion.182
  546.7 9.4 %fusion.183 = bf16[2,512,16,64]{1,3,2,0:T(8,128)(2,1)} fusion(bf16[2,512,16,64]{1,3,2,0:T(8,128)(2,1)} %get-tuple-element.406, s32[]{:T(128)} %get-tuple-element.403, f32[16,512,512]{1,2,0:T(8,128)} %subtract_exponential_fusion.2, bf16[2,512,16,64]{1,3,2,0:T(8,128)(2,1)S(1)} %copy-done.2), kind=kOutput, calls=%fused_computation.37.clone.1 | convolution fusion | flops 541589504 | bytes 18875392 | tf_op jit(solution)/shard_map/while/body/eval_jaxpr/hqk,qhd->khd/dot_general | solution.py:109
  556.2 9.6 %subtract_exponential_fusion.2 = f32[16,512,512]{1,2,0:T(8,128)} fusion(f32[16,512]{1,0:T(8,128)S(1)} %dynamic-slice_bitcast_fusion.2, pred[512]{0:T(512)(128)(4,1)S(1)} %dynamic-slice_reduce_fusion.5, bf16[2,512,16,64]{1,3,2,0:T(8,128)(2,1)} %get-tuple-element.420, s32[]{:T(128)} %get-tuple-element.403, ...), kind=kOutput, calls=%fused_computation.26.clone.1 | convolution fusion | flops 549453824 | bytes 18908672 | tf_op jit(solution)/shard_map/while/body/eval_jaxpr/qhd,khd->hqk/dot_general | solution.py:83
  565.8 10.5 %multiply_reduce_fusion.7 = (f32[16,512]{1,0:T(8,128)S(1)}, f32[16,512,512]{1,2,0:T(8,128)}) fusion(f32[16,512,512]{1,2,0:T(8,128)} %subtract_exponential_fusion.2, bf16[2,512,16,64]{1,3,2,0:T(8,128)(2,1)S(1)} %copy-done.6, s32[]{:T(128)} %get-tuple-element.403, bf16[2,512,16,64]{1,3,2,0:T(8,128)(2,1)S(1)} %copy-done.2), kind=kOutput, calls=%fused_computation.25.clone.1 | convolution fusion | flops 545251328 | bytes 35685376 | tf_op jit(solution)/shard_map/while/body/eval_jaxpr/qhd,khd->hqk/dot_general | solution.py:108
  576.3 11.9 %multiply_convert_fusion.4 = bf16[16,512,512]{1,2,0:T(8,128)(2,1)S(1)} fusion(f32[16,512,512]{1,2,0:T(8,128)} %subtract_exponential_fusion.2, f32[16,512,512]{1,2,0:T(8,128)} %get-tuple-element.366, f32[16,512]{1,0:T(8,128)S(1)} %get-tuple-element.367), kind=kLoop, calls=%fused_computation.24.clone.1 | loop fusion | flops 12582912 | bytes 41975808 | tf_op jit(solution)/shard_map/while/body/eval_jaxpr/convert_element_type | solution.py:116
  588.2 2.6 fusion.182
  593.7 9.4 %fusion.183 = bf16[2,512,16,64]{1,3,2,0:T(8,128)(2,1)} fusion(bf16[2,512,16,64]{1,3,2,0:T(8,128)(2,1)} %get-tuple-element.406, s32[]{:T(128)} %get-tuple-element.403, f32[16,512,512]{1,2,0:T(8,128)} %subtract_exponential_fusion.2, bf16[2,512,16,64]{1,3,2,0:T(8,128)(2,1)S(1)} %copy-done.2), kind=kOutput, calls=%fused_computation.37.clone.1 | convolution fusion | flops 541589504 | bytes 18875392 | tf_op jit(solution)/shard_map/while/body/eval_jaxpr/hqk,qhd->khd/dot_general | solution.py:109
  605.0 6.2 copy.112
  613.3 6.2 copy.114
  619.6 5.5 fusion.82
  625.2 6.6 reshape.201
  631.9 4.7 copy.113
  636.6 6.5 reshape.202
  643.1 6.6 reshape.203
  649.7 12.7 %fusion.83 = bf16[1024,1024]{0,1:T(8,128)(2,1)} fusion(f32[1024,1024]{0,1:T(8,128)} %copy-done.17, bf16[3,1024,1024]{2,1,0:T(8,128)(2,1)} %reshape.185, bf16[1,1024,1024]{2,1,0:T(8,128)(2,1)} %reshape.203, bf16[1,1024,1024]{2,1,0:T(8,128)(2,1)} %reshape.202, bf16[1,1024,1024]{2,1,0:T(8,128)(2,1)S(1)} %copy-done.18), kind=kOutput, calls=%fused_computation.107 | convolution fusion | flops 6450839552 | bytes 18874368 | tf_op jit(solution)/shard_map/mte,mde->td/dot_general | solution.py:241
  662.4 4.1 copy.100
  666.5 2.5 copy.99
  669.2 40.5 %all-reduce = (f32[3,1024]{1,0:T(4,128)}, f32[4096]{0:T(1024)}, f32[1024]{0:T(1024)}, f32[2,1024]{1,0:T(2,128)}, f32[2,1024]{1,0:T(2,128)}) all-reduce(f32[3,1024]{1,0:T(4,128)S(1)} %pad_maximum_fusion, f32[4096]{0:T(1024)S(1)} %copy-done.42, f32[1024]{0:T(1024)S(1)} %get-tuple-element.179, ...), channel_id=1, replica_groups=mesh['dp'=8,'tensor'=4] {'dp','tensor'}, use_global_device_ids=true, to_apply=%region_18.19 | all-reduce | flops 12288 | bytes 98304 | tf_op jit(solution)/shard_map/psum | solution.py:248
  (206 shorter events, 45.0 us)
Async XLA Ops:
  7.2 74.5 %all-gather.14.cloned.1.call-start = ((), (), s32[]{:S(2)}) async-start(), calls=%async_computation.3 | async-start | bytes 2359296 | tf_op jit(solution)/shard_map/all_gather | solution.py:164
  7.9 124.8 %all-gather.18.cloned.1.call-start = ((), (), s32[]{:S(2)}) async-start(), calls=%async_computation.5 | async-start | bytes 2359296 | tf_op jit(solution)/shard_map/all_gather | solution.py:209
  8.6 181.7 %all-gather.10.cloned.1.call-start = ((), (), s32[]{:S(2)}) async-start(), calls=%async_computation.1 | async-start | bytes 2162688 | tf_op jit(solution)/shard_map/all_gather | solution.py:158
  9.4 251.7 %all-gather.8.cloned.1.call-start = ((), (), s32[]{:S(2)}) async-start(), calls=%async_computation | async-start | bytes 6488064 | tf_op jit(solution)/shard_map/all_gather | solution.py:157
  10.0 363.1 %all-gather.12.cloned.1.call-start = ((), (), s32[]{:S(2)}) async-start(), calls=%async_computation.2 | async-start | bytes 10485760 | tf_op jit(solution)/shard_map/all_gather | solution.py:167
  10.0 12.6 %collective-permute-start = (bf16[128,1024]{1,0:T(8,128)(2,1)}, bf16[128,1024]{1,0:T(8,128)(2,1)S(1)}, u32[]{:S(2)}, u32[]{:S(2)}) collective-permute-start(bf16[128,1024]{1,0:T(8,128)(2,1)} %param.24), channel_id=1, source_target_pairs={{0,4},{4,8},{8,12},{12,16},{16,20},{20,24},{24,28},{28,0},{1,5},{5... | collective-permute-start | bytes 786440 | tf_op jit(solution)/shard_map/ppermute | solution.py:31
  22.6 13.8 %collective-permute-start.1 = (bf16[128,1024]{1,0:T(8,128)(2,1)S(1)}, bf16[128,1024]{1,0:T(8,128)(2,1)S(1)}, u32[]{:S(2)}, u32[]{:S(2)}) collective-permute-start(bf16[128,1024]{1,0:T(8,128)(2,1)S(1)} %collective-permute-done), channel_id=1, source_target_pairs={{0,4},{4,8},{8,12},{12,16},{16,20},{20,24},{24,28},{28,0},{1,5},{5... | collective-permute-start | bytes 786440 | tf_op jit(solution)/shard_map/ppermute | solution.py:31
  22.6 15.2 %collective-permute-start.4 = (bf16[128,1024]{1,0:T(8,128)(2,1)}, bf16[128,1024]{1,0:T(8,128)(2,1)S(1)}, u32[]{:S(2)}, u32[]{:S(2)}) collective-permute-start(bf16[128,1024]{1,0:T(8,128)(2,1)} %param.24), channel_id=1, source_target_pairs={{4,0},{8,4},{12,8},{16,12},{20,16},{24,20},{28,24},{0,28},{5,1},{9... | collective-permute-start | bytes 786440 | tf_op jit(solution)/shard_map/ppermute | solution.py:34
  36.4 12.4 %collective-permute-start.2 = (bf16[128,1024]{1,0:T(8,128)(2,1)S(1)}, bf16[128,1024]{1,0:T(8,128)(2,1)S(1)}, u32[]{:S(2)}, u32[]{:S(2)}) collective-permute-start(bf16[128,1024]{1,0:T(8,128)(2,1)S(1)} %collective-permute-done.1), channel_id=1, source_target_pairs={{0,4},{4,8},{8,12},{12,16},{16,20},{20,24},{24,28},{28,0},{1,5},{5... | collective-permute-start | bytes 786440 | tf_op jit(solution)/shard_map/ppermute | solution.py:31
  37.8 16.0 %collective-permute-start.5 = (bf16[128,1024]{1,0:T(8,128)(2,1)S(1)}, bf16[128,1024]{1,0:T(8,128)(2,1)S(1)}, u32[]{:S(2)}, u32[]{:S(2)}) collective-permute-start(bf16[128,1024]{1,0:T(8,128)(2,1)S(1)} %collective-permute-done.4), channel_id=1, source_target_pairs={{4,0},{8,4},{12,8},{16,12},{20,16},{24,20},{28,24},{0,28},{5,1},{9... | collective-permute-start | bytes 786440 | tf_op jit(solution)/shard_map/ppermute | solution.py:34
  48.7 18.3 %collective-permute-start.3 = (bf16[128,1024]{1,0:T(8,128)(2,1)S(1)}, bf16[128,1024]{1,0:T(8,128)(2,1)}, u32[]{:S(2)}, u32[]{:S(2)}) collective-permute-start(bf16[128,1024]{1,0:T(8,128)(2,1)S(1)} %collective-permute-done.2), channel_id=1, source_target_pairs={{0,4},{4,8},{8,12},{12,16},{16,20},{20,24},{24,28},{28,0},{1,5},{5... | collective-permute-start | bytes 786440 | tf_op jit(solution)/shard_map/ppermute | solution.py:31
  53.8 15.4 %collective-permute-start.6 = (bf16[128,1024]{1,0:T(8,128)(2,1)S(1)}, bf16[128,1024]{1,0:T(8,128)(2,1)S(1)}, u32[]{:S(2)}, u32[]{:S(2)}) collective-permute-start(bf16[128,1024]{1,0:T(8,128)(2,1)S(1)} %collective-permute-done.5), channel_id=1, source_target_pairs={{4,0},{8,4},{12,8},{16,12},{20,16},{24,20},{28,24},{0,28},{5,1},{9... | collective-permute-start | bytes 786440 | tf_op jit(solution)/shard_map/ppermute | solution.py:34
  69.2 12.6 %copy-start.34 = (bf16[3,1024]{1,0:T(4,128)(2,1)S(1)}, bf16[3,1024]{1,0:T(4,128)(2,1)}, u32[]{:S(2)}) copy-start(bf16[3,1024]{1,0:T(4,128)(2,1)} %param.26) | copy-start | bytes 18436
  71.2 10.6 %copy-start.19 = (bf16[1024,1024]{1,0:T(8,128)(2,1)S(1)}, bf16[1024,1024]{1,0:T(8,128)(2,1)}, u32[]{:S(2)}) copy-start(bf16[1024,1024]{1,0:T(8,128)(2,1)} %param.18) | copy-start | bytes 6291460
  71.2 13.3 %copy-start.47 = (s32[2,512]{1,0:T(2,128)S(1)}, s32[2,512]{1,0:T(2,128)}, u32[]{:S(2)}) copy-start(s32[2,512]{1,0:T(2,128)} %param.19) | copy-start | bytes 12292
  71.2 13.5 %copy-start.46 = (bf16[4096]{0:T(1024)(128)(2,1)S(1)}, bf16[4096]{0:T(1024)(128)(2,1)}, u32[]{:S(2)}) copy-start(bf16[4096]{0:T(1024)(128)(2,1)} %param.27) | copy-start | bytes 24580
  71.2 14.1 %copy-start.51 = (bf16[1024]{0:T(1024)(128)(2,1)S(1)}, bf16[1024]{0:T(1024)(128)(2,1)}, u32[]{:S(2)}) copy-start(bf16[1024]{0:T(1024)(128)(2,1)} %param.28) | copy-start | bytes 6148
  71.2 319.6 %all-gather.16.cloned.1.call-start = ((), (), s32[]{:S(2)}) async-start(), calls=%async_computation.4 | async-start | bytes 10485760 | tf_op jit(solution)/shard_map/all_gather | solution.py:168
  81.7 388.2 %all-gather.20.cloned.1.call-start = ((), (), s32[]{:S(2)}) async-start(), calls=%async_computation.6 | async-start | bytes 10485760 | tf_op jit(solution)/shard_map/all_gather | solution.py:213
  81.8 8.0 %copy-start.52 = (s32[2]{0:T(128)S(1)}, s32[2]{0:T(128)}, u32[]{:S(2)}) copy-start(s32[2]{0:T(128)} %param.20) | copy-start | bytes 28
  81.8 8.1 %copy-start.43 = (bf16[2,1024]{1,0:T(2,128)(2,1)S(1)}, bf16[2,1024]{1,0:T(2,128)(2,1)}, u32[]{:S(2)}) copy-start(bf16[2,1024]{1,0:T(2,128)(2,1)} %param.21) | copy-start | bytes 12292
  81.8 8.1 %copy-start.44 = (bf16[2,1024]{1,0:T(2,128)(2,1)S(1)}, bf16[2,1024]{1,0:T(2,128)(2,1)}, u32[]{:S(2)}) copy-start(bf16[2,1024]{1,0:T(2,128)(2,1)} %param.29) | copy-start | bytes 12292
  81.8 8.7 %copy-start.45 = (bf16[2,1024]{1,0:T(2,128)(2,1)S(1)}, bf16[2,1024]{1,0:T(2,128)(2,1)}, u32[]{:S(2)}) copy-start(bf16[2,1024]{1,0:T(2,128)(2,1)} %param.30) | copy-start | bytes 12292
  194.5 77.1 %copy-start.22 = (bf16[1024,1024]{0,1:T(8,128)(2,1)S(1)}, bf16[1024,1024]{0,1:T(8,128)(2,1)}, u32[]{:S(2)}) copy-start(bf16[1024,1024]{0,1:T(8,128)(2,1)} %copy.75) | copy-start | bytes 6291460
  339.4 3.9 copy-start.5
  362.4 5.2 copy-start
  362.4 5.2 copy-start.24
  362.4 5.2 copy-start.26
  362.4 5.2 copy-start.20
  362.4 5.2 copy-start.23
  373.1 17.7 %copy-start.41 = (f32[4096]{0:T(1024)S(1)}, f32[4096]{0:T(1024)}, u32[]{:S(2)}) copy-start(f32[4096]{0:T(1024)} %convert_element_type.124) | copy-start | bytes 49156
  373.1 17.7 %copy-start.48 = (f32[1024]{0:T(1024)S(1)}, f32[1024]{0:T(1024)}, u32[]{:S(2)}) copy-start(f32[1024]{0:T(1024)} %convert_element_type.126) | copy-start | bytes 12292
  390.8 55.5 %copy-start.9 = (bf16[1024,1024]{0,1:T(8,128)(2,1)S(1)}, bf16[1024,1024]{0,1:T(8,128)(2,1)}, u32[]{:S(2)}) copy-start(bf16[1024,1024]{0,1:T(8,128)(2,1)} %copy.85) | copy-start | bytes 6291460
  443.5 26.4 %copy-start.28 = (f32[1024]{0:T(1024)}, f32[1024]{0:T(1024)S(1)}, u32[]{:S(2)}) copy-start(f32[1024]{0:T(1024)S(1)} %broadcast_multiply_fusion.4) | copy-start | bytes 12292
  446.3 23.6 %copy-start.30 = (f32[1024]{0:T(1024)}, f32[1024]{0:T(1024)S(1)}, u32[]{:S(2)}) copy-start(f32[1024]{0:T(1024)S(1)} %add_rsqrt_fusion) | copy-start | bytes 12292
  447.9 22.0 %copy-start.37 = (f32[1024]{0:T(1024)}, f32[1024]{0:T(1024)S(1)}, u32[]{:S(2)}) copy-start(f32[1024]{0:T(1024)S(1)} %get-tuple-element.250) | copy-start | bytes 12292
  448.0 21.9 %copy-start.39 = (f32[1024]{0:T(1024)}, f32[1024]{0:T(1024)S(1)}, u32[]{:S(2)}) copy-start(f32[1024]{0:T(1024)S(1)} %get-tuple-element.251) | copy-start | bytes 12292
  469.9 18.7 %copy-start.12 = (f32[1024,1024]{0,1:T(8,128)S(1)}, f32[1024,1024]{0,1:T(8,128)}, u32[]{:S(2)}) copy-start(f32[1024,1024]{0,1:T(8,128)} %copy-done.11) | copy-start | bytes 12582916
  488.6 4.1 copy-start.21
  504.6 4.7 copy-start.1
  504.6 4.7 copy-start.25
  504.6 4.7 copy-start.27
  509.3 9.6 %copy-start.2 = (bf16[2,512,16,64]{1,3,2,0:T(8,128)(2,1)S(1)}, bf16[2,512,16,64]{1,3,2,0:T(8,128)(2,1)}, u32[]{:S(2)}) copy-start(bf16[2,512,16,64]{1,3,2,0:T(8,128)(2,1)} %get-tuple-element.422) | copy-start | bytes 6291460 | tf_op jit(solution)/shard_map/while
  509.3 9.6 %copy-start.6 = (bf16[2,512,16,64]{1,3,2,0:T(8,128)(2,1)S(1)}, bf16[2,512,16,64]{1,3,2,0:T(8,128)(2,1)}, u32[]{:S(2)}) copy-start(bf16[2,512,16,64]{1,3,2,0:T(8,128)(2,1)} %get-tuple-element.423) | copy-start | bytes 6291460 | tf_op jit(solution)/shard_map/while
  529.4 11.9 %copy-start.3 = (bf16[2,512,16,64]{1,3,2,0:T(8,128)(2,1)S(1)}, bf16[2,512,16,64]{1,3,2,0:T(8,128)(2,1)}, u32[]{:S(2)}) copy-start(bf16[2,512,16,64]{1,3,2,0:T(8,128)(2,1)} %get-tuple-element.420) | copy-start | bytes 6291460 | tf_op jit(solution)/shard_map/while
  529.4 11.9 %copy-start.13 = (bf16[2,512,16,64]{1,3,2,0:T(8,128)(2,1)S(1)}, bf16[2,512,16,64]{1,3,2,0:T(8,128)(2,1)}, u32[]{:S(2)}) copy-start(bf16[2,512,16,64]{1,3,2,0:T(8,128)(2,1)} %get-tuple-element.405) | copy-start | bytes 6291460 | tf_op jit(solution)/shard_map/while
  556.2 9.6 %copy-start.2 = (bf16[2,512,16,64]{1,3,2,0:T(8,128)(2,1)S(1)}, bf16[2,512,16,64]{1,3,2,0:T(8,128)(2,1)}, u32[]{:S(2)}) copy-start(bf16[2,512,16,64]{1,3,2,0:T(8,128)(2,1)} %get-tuple-element.422) | copy-start | bytes 6291460 | tf_op jit(solution)/shard_map/while
  556.2 9.6 %copy-start.6 = (bf16[2,512,16,64]{1,3,2,0:T(8,128)(2,1)S(1)}, bf16[2,512,16,64]{1,3,2,0:T(8,128)(2,1)}, u32[]{:S(2)}) copy-start(bf16[2,512,16,64]{1,3,2,0:T(8,128)(2,1)} %get-tuple-element.423) | copy-start | bytes 6291460 | tf_op jit(solution)/shard_map/while
  576.3 11.9 %copy-start.3 = (bf16[2,512,16,64]{1,3,2,0:T(8,128)(2,1)S(1)}, bf16[2,512,16,64]{1,3,2,0:T(8,128)(2,1)}, u32[]{:S(2)}) copy-start(bf16[2,512,16,64]{1,3,2,0:T(8,128)(2,1)} %get-tuple-element.420) | copy-start | bytes 6291460 | tf_op jit(solution)/shard_map/while
  576.3 11.9 %copy-start.13 = (bf16[2,512,16,64]{1,3,2,0:T(8,128)(2,1)S(1)}, bf16[2,512,16,64]{1,3,2,0:T(8,128)(2,1)}, u32[]{:S(2)}) copy-start(bf16[2,512,16,64]{1,3,2,0:T(8,128)(2,1)} %get-tuple-element.405) | copy-start | bytes 6291460 | tf_op jit(solution)/shard_map/while
  611.2 8.4 %copy-start.10 = (bf16[1024,1024]{0,1:T(8,128)(2,1)S(1)}, bf16[1024,1024]{0,1:T(8,128)(2,1)}, u32[]{:S(2)}) copy-start(bf16[1024,1024]{0,1:T(8,128)(2,1)} %copy.85) | copy-start | bytes 6291460
  611.2 8.4 %copy-start.29 = (f32[1024]{0:T(1024)S(1)}, f32[1024]{0:T(1024)}, u32[]{:S(2)}) copy-start(f32[1024]{0:T(1024)} %copy-done.28) | copy-start | bytes 12292
  611.2 8.4 %copy-start.31 = (f32[1024]{0:T(1024)S(1)}, f32[1024]{0:T(1024)}, u32[]{:S(2)}) copy-start(f32[1024]{0:T(1024)} %copy-done.30) | copy-start | bytes 12292
  611.2 8.4 %copy-start.33 = (f32[1,1024]{1,0:T(1,128)S(1)}, f32[1,1024]{1,0:T(1,128)}, u32[]{:S(2)}) copy-start(f32[1,1024]{1,0:T(1,128)} %get-tuple-element.237) | copy-start | bytes 12292
  611.2 8.4 %copy-start.36 = (f32[1,1024]{1,0:T(1,128)S(1)}, f32[1,1024]{1,0:T(1,128)}, u32[]{:S(2)}) copy-start(f32[1,1024]{1,0:T(1,128)} %get-tuple-element.239) | copy-start | bytes 12292
  611.2 8.4 %copy-start.38 = (f32[1024]{0:T(1024)S(1)}, f32[1024]{0:T(1024)}, u32[]{:S(2)}) copy-start(f32[1024]{0:T(1024)} %copy-done.37) | copy-start | bytes 12292
  611.2 8.4 %copy-start.40 = (f32[1024]{0:T(1024)S(1)}, f32[1024]{0:T(1024)}, u32[]{:S(2)}) copy-start(f32[1024]{0:T(1024)} %copy-done.39) | copy-start | bytes 12292
  625.1 6.8 copy-start.15
  643.1 6.6 copy-start.18
  662.4 4.1 copy-start.16
  662.4 6.7 copy-start.50
  662.4 6.7 copy-start.49
  662.4 6.7 copy-start.35
  662.4 6.7 copy-start.42
  (11 other events, 25.8 us)
Sparse Core Ops, SparseCore 0:
  10.0 71.6 all-gather.13
  83.8 48.8 all-gather.17
  135.6 54.7 all-gather.9
  193.1 67.9 all-gather.7
  263.1 56.7 all-gather.11
  321.4 58.2 all-gather.15
  381.2 58.2 all-gather.19
